TPU v7x, 128 devices: a 2x2x16 block of a 8x8x16 slice. The times are simulated.
128 devices in a mesh: kpt: 4 (over x, y), row: 16 (over z), col: 2 (over core).
Axes of the slice: x: 2, y: 2, z: 16, core: 2. Of those that a mesh axis runs over, the one named last changes fastest.
The devices are a block of a 8x8x16 slice.
Arguments:
- wannier: float32 [128, 32, 1024], P('kpt', ('row', 'col')), parts along dimension 0, may hold values from -6 to 6
- pairs: int32 [384, 2], replicated, may hold values from 0 to 31, as said below
- gmap: int32 [8192], replicated, may hold values from 1 to 32767, as said below
- screened: bfloat16 [8, 2, 8192, 8192], P('kpt', None, 'row', 'col'), parts along dimension 0, may hold values from -0.046875 to 0.046875
Outputs:
- coulomb: float32 [2, 2, 1536, 384], P(None, None, ('kpt', 'row', 'col')), parts along dimension 2
There are 4 independent parts, one for each index of `kpt`. A program takes and returns all parts, laid end to end along the dimension named above; an argument that names none is the same for every part. Nothing has to cross between parts.
Inputs may be any that keep to these rules, and one draw needn't show every extreme that they name: `gmap`: 8192 distinct flat cells of the grid; cell 0 is never among them. `pairs`: in each row the first Wannier function is no greater than the second; no two rows are equal.
All inputs are finite; a program needn't handle non-finite values.
Results may differ from a plain program's by a relative error of at most 0.0082.
Values may be sent and summed in bfloat16 or wider, within the bound.
A program may use at most 128 MiB of HBM per device.

v0:
```python
import math

import jax
import jax.numpy as jnp
from jax import lax
from jax.sharding import PartitionSpec as P

NW = 32
GX = 32
NG = 8192
NP = 384


def from_partner(value, axis, stride):
    return lax.ppermute(value, axis, [(i, i ^ 1 << stride) for i in range(lax.axis_size(axis))])


def in_blocks(value, dim, size):
    before, after = (value.shape[:dim], value.shape[dim + 1 :])
    return jnp.moveaxis(value.reshape(*before, size, -1, *after), dim, 0)


def sum_at_owner(value, axis, dim):
    pieces = in_blocks(value, dim, lax.axis_size(axis))
    arrived = lax.all_to_all(pieces, axis, split_axis=0, concat_axis=0, tiled=True)
    return arrived.astype(jnp.float32).sum(axis=0)


def line_tables(side_len):
    positions = jnp.arange(side_len, dtype=jnp.int32)
    phase_index = positions[:, None] * positions[None, :] % side_len
    angles = phase_index.astype(jnp.float32) * (2.0 * math.pi / side_len)
    return (jnp.cos(angles), jnp.sin(angles))


def plane_transform(density):
    cosine, sine_table = line_tables(GX)
    highest = lax.Precision.HIGHEST
    shaped = density.reshape(-1, GX, GX)
    real_z = jnp.einsum("nyz,kz->nyk", shaped, cosine, precision=highest)
    imag_z = -jnp.einsum("nyz,kz->nyk", shaped, sine_table, precision=highest)
    new_real = jnp.einsum("jy,nyk->njk", cosine, real_z, precision=highest) + jnp.einsum(
        "jy,nyk->njk", sine_table, imag_z, precision=highest
    )
    new_imag = jnp.einsum("jy,nyk->njk", cosine, imag_z, precision=highest) - jnp.einsum(
        "jy,nyk->njk", sine_table, real_z, precision=highest
    )
    return (new_real.reshape(density.shape), new_imag.reshape(density.shape))


def line_transform(real_part, imag_part):
    cosine, sine_table = line_tables(GX)
    highest = lax.Precision.HIGHEST
    new_real = jnp.einsum("kn,pny->pky", cosine, real_part, precision=highest) + jnp.einsum(
        "kn,pny->pky", sine_table, imag_part, precision=highest
    )
    new_imag = jnp.einsum("kn,pny->pky", cosine, imag_part, precision=highest) - jnp.einsum(
        "kn,pny->pky", sine_table, real_part, precision=highest
    )
    return (new_real, new_imag)


def right_columns(screened, segment):
    w_real = screened[:, 0]
    w_imag = screened[:, 1]
    real_real = jnp.einsum("fgh,bh->fgb", w_real, segment[0], preferred_element_type=jnp.float32)
    imag_imag = jnp.einsum("fgh,bh->fgb", w_imag, segment[1], preferred_element_type=jnp.float32)
    real_imag = jnp.einsum("fgh,bh->fgb", w_real, segment[1], preferred_element_type=jnp.float32)
    imag_real = jnp.einsum("fgh,bh->fgb", w_imag, segment[0], preferred_element_type=jnp.float32)
    return jnp.stack([real_real - imag_imag, real_imag + imag_real], axis=1)


def shards(wannier, pairs, gmap, screened):
    planes = wannier.shape[1]
    grid_cells = wannier.shape[2]
    members = jnp.arange(NW, dtype=jnp.int32)[None, :]
    pick_first = (pairs[:, 0:1] == members).astype(jnp.float32)
    pick_second = (pairs[:, 1:2] == members).astype(jnp.float32)
    flat_rows = wannier.reshape(NW, -1)
    highest = lax.Precision.HIGHEST
    density = jnp.dot(pick_first, flat_rows, precision=highest) * jnp.dot(
        pick_second, flat_rows, precision=highest
    )
    density = density.reshape(NP, planes, grid_cells)
    arrived = lax.all_to_all(
        density.astype(jnp.bfloat16), ("row", "col"), split_axis=0, concat_axis=1, tiled=True
    ).astype(density.dtype)
    real_part, imag_part = plane_transform(arrived)
    real_part, imag_part = line_transform(real_part, imag_part)
    owned = real_part.shape[0]
    norm_factor = 1.0 / math.sqrt(GX * GX * GX)
    rho_real = jnp.take(real_part.reshape(owned, -1), gmap, axis=1) * norm_factor
    rho_imag = jnp.take(imag_part.reshape(owned, -1), gmap, axis=1) * norm_factor
    rho = jnp.stack([rho_real, rho_imag], axis=0).astype(jnp.bfloat16)
    row_span = screened.shape[2]
    col_span = screened.shape[3]
    halves = lax.all_to_all(rho, "col", split_axis=2, concat_axis=1, tiled=True)
    right_panel = lax.all_gather(halves, "row", axis=1, tiled=True)
    screened_rho = right_columns(screened, right_panel)
    row_start = lax.axis_index("row") * row_span
    col_index = lax.axis_index("col")
    owner_col = row_start // col_span
    offset = jnp.clip(row_start - col_index * col_span, 0, col_span - row_span)
    local_block = lax.dynamic_slice_in_dim(right_panel, offset, row_span, 2)
    partner = from_partner(local_block, "col", 0)
    left_panel = jnp.where(owner_col == col_index, local_block, partner)
    left_wide = left_panel.astype(jnp.float32)
    u_real = jnp.einsum(
        "ag,fgb->fab", left_wide[0], screened_rho[:, 0], precision=highest
    ) + jnp.einsum("ag,fgb->fab", left_wide[1], screened_rho[:, 1], precision=highest)
    u_imag = jnp.einsum(
        "ag,fgb->fab", left_wide[0], screened_rho[:, 1], precision=highest
    ) - jnp.einsum("ag,fgb->fab", left_wide[1], screened_rho[:, 0], precision=highest)
    partial_terms = jnp.stack([u_real, u_imag], axis=1) / math.sqrt(NG)
    return sum_at_owner(partial_terms.astype(jnp.bfloat16), ("row", "col"), 2)


def solution(mesh):
    return jax.shard_map(
        shards,
        mesh=mesh,
        in_specs=(P("kpt", ("row", "col"), None), P(), P(), P("kpt", None, "row", "col")),
        out_specs=P(None, None, ("kpt", "row", "col"), None),
        check_vma=False,
    )
```

profile of v0, /device:TPU:69, one launch (start us, length us, event | category | flops | bytes accessed | tf_op | source)
XLA Modules:
  0.0 495.3 jit_solution(486574713012958751)
XLA Ops:
  6.5 0.8 slice_reduce_fusion
  7.3 1.7 fusion.51
  9.1 0.0 copy-done.2
  9.1 0.8 fusion.49
  9.9 0.5 broadcast.117
  10.4 1.2 reduce.5
  11.7 0.0 copy-start.3
  11.7 1.4 reshape.69
  13.0 18.5 %all-to-all-start = ((bf16[32,2,6144]{2,1,0:T(2,128)(2,1)}), bf16[32,2,6144]{2,1,0:T(2,128)(2,1)S(1)}, u32[]{:S(2)}, u32[]{:S(2)}) async-start(bf16[32,2,6144]{2,1,0:T(2,128)(2,1)} %reshape.69), calls=%async_computation | async-start | bytes 1572864 | tf_op jit(solution)/shard_map/all_to_all | solution.py:85
  31.6 0.1 all-gather.2.cloned.1.call-start
  31.7 44.3 %all-to-all-done = bf16[32,2,6144]{2,1,0:T(2,128)(2,1)S(1)} async-done(((bf16[32,2,6144]{2,1,0:T(2,128)(2,1)}), bf16[32,2,6144]{2,1,0:T(2,128)(2,1)S(1)}, u32[]{:S(2)}, u32[]{:S(2)}) %all-to-all-start) | async-done | bytes 786464 | tf_op jit(solution)/shard_map/all_to_all | solution.py:85
  76.0 0.7 reshape.70
  76.7 4.6 reduce.2
  81.3 0.2 all_to_all.28
  81.5 5.1 %copy.127 = bf16[12,32,1,1024]{1,0,3,2:T(8,128)(2,1)} copy(bf16[12,32,1,1024]{3,0,1,2:T(8,128)(2,1)S(1)} %bitcast.146) | data formatting | bytes 1572864 | tf_op jit(solution)/shard_map/reshape | solution.py:39
  86.6 5.4 %reshape.65 = bf16[384,32,32]{0,2,1:T(8,128)(2,1)S(1)} reshape(bf16[12,32,1,1024]{1,0,3,2:T(8,128)(2,1)} %copy.127) | data formatting | bytes 1572864 | tf_op jit(solution)/shard_map/reshape | solution.py:39
  92.0 0.8 convolution_negate_fusion
  92.9 0.8 fusion.73
  93.7 2.5 fusion.25
  96.2 3.7 fusion.29
  99.9 2.5 subtract_bitcast_fusion.1
  102.3 6.0 %copy.103 = f32[384,32,32]{2,1,0:T(8,128)} copy(f32[384,32,32]{0,1,2:T(8,128)S(1)} %subtract_bitcast_fusion.1) | data formatting | bytes 3145728 | tf_op jit(solution)/shard_map/sub | solution.py:45
  108.3 5.4 %reshape.34 = f32[12,32,1024]{2,1,0:T(8,128)S(1)} reshape(f32[384,32,32]{2,1,0:T(8,128)} %copy.103) | data formatting | bytes 3145728 | tf_op jit(solution)/shard_map/reshape | solution.py:48
  113.8 2.8 fusion.67
  116.5 3.7 add_bitcast_fusion.1
  120.2 6.9 %copy.100 = f32[384,32,32]{2,1,0:T(8,128)} copy(f32[384,32,32]{0,1,2:T(8,128)} %add_bitcast_fusion.1) | data formatting | bytes 3145728 | tf_op jit(solution)/shard_map/add | solution.py:42
  127.1 5.0 %reshape.33 = f32[12,32,1024]{2,1,0:T(8,128)S(1)} reshape(f32[384,32,32]{2,1,0:T(8,128)} %copy.100) | data formatting | bytes 3145728 | tf_op jit(solution)/shard_map/reshape | solution.py:48
  132.2 2.8 fusion.70
  134.9 2.8 subtract_bitcast_fusion
  137.7 10.1 %copy.126 = f32[12,32,1024]{0,2,1:T(8,128)} copy(f32[12,32,1024]{2,1,0:T(8,128)} %subtract_bitcast_fusion) | data formatting | bytes 3145728 | tf_op jit(solution)/shard_map/reshape | solution.py:93
  147.8 3.1 add_bitcast_fusion
  150.9 8.9 %copy.125 = f32[12,32,1024]{0,2,1:T(8,128)} copy(f32[12,32,1024]{2,1,0:T(8,128)S(1)} %add_bitcast_fusion) | data formatting | bytes 3145728 | tf_op jit(solution)/shard_map/reshape | solution.py:92
  159.9 33.5 %gather_fusion.1 = f32[8192,12]{1,0:T(8,128)} fusion(f32[12,32768]{0,1:T(8,128)} %bitcast.140, s32[8192]{0:T(1024)S(1)} %fusion.58), kind=kCustom, calls=%fused_computation.1.clone | custom fusion | bytes 819200 | tf_op jit(solution)/shard_map/jit(_take)/gather | solution.py:93
  193.4 33.5 %gather_fusion = f32[8192,12]{1,0:T(8,128)} fusion(f32[12,32768]{0,1:T(8,128)} %bitcast.141, s32[8192]{0:T(1024)S(1)} %fusion.58), kind=kCustom, calls=%fused_computation.clone | custom fusion | bytes 819200 | tf_op jit(solution)/shard_map/jit(_take)/gather | solution.py:92
  226.9 6.8 %fusion.15 = (bf16[1,12,8192]{1,2,0:T(8,128)(2,1)S(1)}, bf16[1,12,8192]{1,2,0:T(8,128)(2,1)S(1)}) fusion(f32[8192,12]{1,0:T(8,128)} %gather_fusion, pred[8192]{0:T(1024)(128)(4,1)S(1)} %compare_and_fusion, f32[8192,12]{1,0:T(8,128)} %gather_fusion.1), kind=kLoop, calls=%fused_computation.24 | loop fusion | flops 589824 | bytes 1187840 | tf_op jit(solution)/shard_map/stack | solution.py:94
  233.6 0.9 pad_maximum_fusion
  234.6 35.4 %copy.153 = bf16[2,12,8192]{1,0,2:T(2,128)(2,1)} copy(bf16[2,12,8192]{1,2,0:T(8,128)(2,1)S(1)} %pad_maximum_fusion) | data formatting | bytes 786432 | tf_op jit(solution)/shard_map/stack | solution.py:94
  270.0 10.1 %reshape.71 = bf16[2,2,49152]{2,1,0:T(2,128)(2,1)S(1)} reshape(bf16[8192,2,12]{2,1,0:T(2,128)(2,1)} %bitcast.142) | data formatting | bytes 786432
  280.1 4.4 all_to_all.38
  284.5 10.9 %reshape.72 = bf16[8192,2,12]{2,1,0:T(2,128)(2,1)} reshape(bf16[2,2,49152]{2,1,0:T(2,128)(2,1)S(1)} %all_to_all.38) | data formatting | bytes 786432
  295.5 9.0 %copy.107 = bf16[2,12,2,4096]{3,0,1,2:T(2,128)(2,1)S(1)} copy(bf16[2,12,2,4096]{1,0,3,2:T(2,128)(2,1)} %bitcast.143) | data formatting | bytes 786432 | tf_op jit(solution)/shard_map/all_to_all | solution.py:97
  304.5 1.0 copy.108
  305.5 0.1 all-gather.2.cloned.1.call-update
  305.5 70.5 %all-gather.2.cloned.1.call-done = bf16[2,384,4096]{2,1,0:T(8,128)(2,1)} async-done(((bf16[2,24,4096]{2,1,0:T(8,128)(2,1)}), bf16[2,384,4096]{2,1,0:T(8,128)(2,1)}) %all-gather.2.cloned.1.call-update) | async-done | bytes 6291472 | tf_op jit(solution)/shard_map/all_gather | solution.py:98
  376.0 1.7 constant_dynamic-slice_fusion
  377.7 0.0 slice-start.1
  377.7 4.6 collective-permute-start
  382.3 6.9 %fusion = f32[384,2,512]{2,0,1:T(8,128)S(1)} fusion(bf16[2,2,512,4096]{3,2,1,0:T(8,128)(2,1)} %param.9, bf16[2,384,4096]{2,1,0:T(8,128)(2,1)} %all-gather.2.cloned.1.call-done), kind=kOutput, calls=%fused_computation.2 | convolution fusion | flops 3221225472 | bytes 13107200 | tf_op jit(solution)/shard_map/fgh,bh->fgb/dot_general | solution.py:69
  389.2 5.9 %fusion.2 = f32[384,2,512]{2,0,1:T(8,128)S(1)} fusion(bf16[2,2,512,4096]{3,2,1,0:T(8,128)(2,1)} %param.9, bf16[2,384,4096]{2,1,0:T(8,128)(2,1)S(1)} %bitcast.149), kind=kOutput, calls=%fused_computation.4 | convolution fusion | flops 3221225472 | bytes 13107200 | tf_op jit(solution)/shard_map/fgh,bh->fgb/dot_general | solution.py:67
  395.1 5.9 %fusion.34 = f32[384,2,512]{2,0,1:T(8,128)S(1)} fusion(f32[384,2,512]{2,0,1:T(8,128)S(1)} %fusion, bf16[2,2,512,4096]{3,2,1,0:T(8,128)(2,1)} %param.9, bf16[2,384,4096]{2,1,0:T(8,128)(2,1)S(1)} %bitcast.149), kind=kOutput, calls=%fused_computation.47 | convolution fusion | flops 3221618688 | bytes 14680064 | tf_op jit(solution)/shard_map/fgh,bh->fgb/dot_general | solution.py:68
  401.1 6.2 %fusion.31 = f32[384,2,512]{2,0,1:T(8,128)S(1)} fusion(f32[384,2,512]{2,0,1:T(8,128)S(1)} %fusion.2, bf16[2,2,512,4096]{3,2,1,0:T(8,128)(2,1)} %param.9, bf16[2,384,4096]{2,1,0:T(8,128)(2,1)S(1)} %bitcast.149), kind=kOutput, calls=%fused_computation.46 | convolution fusion | flops 3221618688 | bytes 14680064 | tf_op jit(solution)/shard_map/fgh,bh->fgb/dot_general | solution.py:66
  407.3 0.0 collective-permute-done
  407.3 0.5 broadcast_select_fusion
  407.8 1.2 fusion.19
  409.1 1.2 fusion.21
  410.3 1.2 fusion.46
  411.5 0.9 copy.113
  412.4 1.2 fusion.43
  413.7 0.9 copy.116
  414.6 1.6 fusion.50
  416.1 0.8 copy.117
  417.0 70.0 %all_to_all.39 = bf16[32,2,2,12,384]{4,1,3,2,0:T(2,128)(2,1)S(1)} all-to-all(bf16[32,2,2,12,384]{4,1,3,2,0:T(2,128)(2,1)S(1)} %copy.117), channel_id=1, replica_groups=mesh['kpt'=4,'row'=16,'col'=2] {'row','col'}, dimensions={0} | all-to-all | bytes 2359296 | tf_op jit(solution)/shard_map/all_to_all | solution.py:25
  487.0 0.4 convert_reduce_fusion
  487.4 0.7 copy.120
  (12 shorter events, 0.0 us)
Async XLA Ops:
  6.5 2.5 copy-start.2
  11.7 20.0 %copy-start.3 = (s32[8192]{0:T(1024)S(1)}, s32[8192]{0:T(1024)}, u32[]{:S(2)}) copy-start(s32[8192]{0:T(1024)} %param.8) | copy-start | bytes 98308
  13.0 62.9 %all-to-all-start = ((bf16[32,2,6144]{2,1,0:T(2,128)(2,1)}), bf16[32,2,6144]{2,1,0:T(2,128)(2,1)S(1)}, u32[]{:S(2)}, u32[]{:S(2)}) async-start(bf16[32,2,6144]{2,1,0:T(2,128)(2,1)} %reshape.69), calls=%async_computation | async-start | bytes 1572864 | tf_op jit(solution)/shard_map/all_to_all | solution.py:85
  31.6 344.5 %all-gather.2.cloned.1.call-start = ((), (), s32[]{:S(2)}) async-start(), calls=%async_computation.3 | async-start | bytes 6684672 | tf_op jit(solution)/shard_map/all_gather | solution.py:98
  113.7 2.8 copy-start
  132.1 2.8 copy-start.1
  376.0 13.2 %slice-start = ((s8[6291456]{0:T(1024)(128)(4,1)}), s8[4194304]{0:T(1024)(128)(4,1)S(1)}, s32[]{:S(2)}) async-start(s8[6291456]{0:T(1024)(128)(4,1)} %bitcast.148), calls=%async_computation.4 | async-start | bytes 8388608
  377.7 11.5 %slice-start.1 = ((s8[6291456]{0:T(1024)(128)(4,1)}), s8[2097152]{0:T(1024)(128)(4,1)S(1)}, s32[]{:S(2)}) async-start(s8[6291456]{0:T(1024)(128)(4,1)} %bitcast.148), calls=%async_computation.5 | async-start | bytes 4194304
  377.7 29.6 %collective-permute-start = (bf16[2,384,512]{2,1,0:T(8,128)(2,1)S(1)}, bf16[2,384,512]{2,1,0:T(8,128)(2,1)S(1)}, u32[]{:S(2)}, u32[]{:S(2)}) collective-permute-start(bf16[2,384,512]{2,1,0:T(8,128)(2,1)S(1)} %constant_dynamic-slice_fusion), channel_id=1, source_target_pairs={{0,1},{1,0},{2,3},{3,2},{4,5},{5,4},{6,7},{7,6},{8,9},{9,8},{10,11... | collective-permute-start | bytes 2359304 | tf_op jit(solution)/shard_map/ppermute | solution.py:15
Sparse Core Ops, SparseCore 0:
  305.6 70.3 all-gather.1
where the time goes:
time: 504 us; the launch traced here: 495 us
  local copies, waits for them, and re-layouts  195 us (39%)
  waiting for transfers between devices  115 us (23%)
  blocking collectives  74.4 us (15%)
  matrix products  57.8 us (11%)
  starting transfers between devices  23.2 us (5%)
  other arithmetic  16 us (3%)
  between operations  14.2 us (3%)
    all_gather x1, waiting for transfers between devices, shards(): right_panel = lax.all_gather(halves, 'row', axis=1, tiled=True)  70.5 us
    all_to_all x1, blocking collectives, sum_at_owner(): lax.all_to_all(pieces, axis, split_axis=0, concat_axis=0, tiled=True)  70 us
    all_to_all x1, waiting for transfers between devices, shards(): lax.all_to_all(density.astype(jnp.bfloat16), ('row', 'col'), split_axis=0...  44.3 us
    another operation x1, local copies, waits for them, and re-layouts, shards(): rho = jnp.stack([rho_real, rho_imag], axis=0).astype(jnp.bfloat16)  35.4 us
    gather x1, local copies, waits for them, and re-layouts, shards(): jnp.take(imag_part.reshape(owned, -1), gmap, axis=1) * norm_factor  33.5 us
    gather x1, local copies, waits for them, and re-layouts, shards(): jnp.take(real_part.reshape(owned, -1), gmap, axis=1) * norm_factor  33.5 us
    unnamed x16, local copies, waits for them, and re-layouts  23.2 us
    all_to_all x1, starting transfers between devices, shards(): lax.all_to_all(density.astype(jnp.bfloat16), ('row', 'col'), split_axis=0...  18.5 us
  transfers between devices with their start and end apart: 3, of which 2 were waited for; matrix products, arithmetic and copies ran while one was open for 5% of the time, Pallas kernels for 0%

commit v1 on v0

v1 whole, which is shorter than its diff:
```python
import functools
import math

import jax
import jax.numpy as jnp
from jax import lax
from jax.experimental import pallas as pl
from jax.experimental.pallas import tpu as pltpu
from jax.sharding import PartitionSpec as P

MESH = pl.DeviceIdType.MESH
GX = 32
F32 = jnp.float32
BF16 = jnp.bfloat16


def dot(a, b):
    return lax.dot_general(a, b, (((1,), (0,)), ((), ())), preferred_element_type=F32)


def dot_tn(a, b):
    return lax.dot_general(a, b, (((0,), (0,)), ((), ())), preferred_element_type=F32)


def greet(targets):
    barrier = pltpu.get_barrier_semaphore()
    for target in targets:
        pl.semaphore_signal(barrier, inc=1, device_id=target, device_id_type=MESH)
    pl.semaphore_wait(barrier, len(targets))


class Ring:
    def __init__(self, n, own_ref, slot_ref, send_sems, recv_sems):
        self.n, self.half = n, n // 2
        self.own, self.slot = own_ref, slot_ref
        self.send_sems, self.recv_sems = send_sems, recv_sems
        self.me = lax.axis_index("row")
        self.rows = own_ref.shape[0] // 2

    def owner(self, way, step):
        return lax.rem(self.me + step + self.n, self.n) if way else lax.rem(self.me - step + self.n, self.n)

    def copy(self, way, chunk, step, first, arriving=False):
        span = pl.ds(chunk * self.rows, self.rows)
        place = self.slot(self.owner(way, step + 1 if arriving else step)).at[span]
        source = self.own.at[span] if first else place
        target = self.owner(way, -1)
        return pltpu.make_async_remote_copy(
            src_ref=source,
            dst_ref=place,
            send_sem=self.send_sems.at[way, chunk, step],
            recv_sem=self.recv_sems.at[way, chunk, step],
            device_id={"row": self.owner(1 - way, 1)},
            device_id_type=MESH,
        )

    def run(self, on_block, before=None):
        last = self.half - 1
        for way in range(2):
            for chunk in range(2):
                self.copy(way, chunk, 0, True).start()
        if before is not None:
            before()

        def step_body(step, _):
            for chunk in range(2):
                for way in range(2):
                    self.copy(way, chunk, step - 1, False, True).wait_recv()
                    self.copy(way, chunk, step, False).start()
            on_block(self.owner(0, step))
            on_block(self.owner(1, step))
            return 0

        lax.fori_loop(1, last, step_body, 0)
        for chunk in range(2):
            for way in range(2):
                self.copy(way, chunk, last - 1, False, True).wait_recv()
                if way == chunk:
                    self.copy(way, chunk, last, False).start()
        on_block(self.owner(0, last))
        on_block(self.owner(1, last))
        for way in range(2):
            self.copy(way, way, last, False, True).wait_recv()
        on_block(self.owner(0, self.half))

    def drain(self):
        for way in range(2):
            for chunk in range(2):
                self.copy(way, chunk, 0, True).wait_send()

        def body(step, _):
            for way in range(2):
                for chunk in range(2):
                    self.copy(way, chunk, step, False).wait_send()
            return 0

        lax.fori_loop(1, self.half - 1, body, 0)
        for way in range(2):
            self.copy(way, way, self.half - 1, False).wait_send()


def neighbours(n, cols):
    row, col = lax.axis_index("row"), lax.axis_index("col")
    right, left = lax.rem(row + 1, n), lax.rem(row + n - 1, n)
    return [{"row": right}, {"row": left}, {"col": 1 - col}]


def planes_kernel(n, own_ref, out_ref, send_sems, recv_sems, pair_send, pair_recv):
    row, col = lax.axis_index("row"), lax.axis_index("col")
    greet(neighbours(n, 2))

    def slot(owner):
        return out_ref.at[owner * 2 + col]

    def pair_copy(source, owner, to_col):
        return pltpu.make_async_remote_copy(
            src_ref=source,
            dst_ref=out_ref.at[owner * 2 + to_col],
            send_sem=pair_send.at[owner],
            recv_sem=pair_recv.at[owner],
            device_id={"col": 1 - col},
            device_id_type=MESH,
        )

    ring = Ring(n, own_ref, slot, send_sems, recv_sems)

    def before():
        pair_copy(own_ref, row, col).start()
        out_ref[row * 2 + col] = own_ref[...]

    def on_block(owner):
        pair_copy(slot(owner), owner, col).start()

    ring.run(on_block, before)
    ring.drain()

    def finish(owner, _):
        pair_copy(slot(owner), owner, col).wait_send()
        pair_copy(slot(owner), owner, 1 - col).wait_recv()
        return 0

    lax.fori_loop(0, n, finish, 0)


def wave_kernel(pair_tiles, w_ref, pick_ref, cos_ref, sin_ref, turn_ref, out_ref, even0, odd0, even1, odd1, acc_re, acc_im):
    side = w_ref.shape[0]
    rows = w_ref.shape[1]

    def densities(x, even, odd):
        plane = w_ref[x].astype(F32)
        for tile in range(pair_tiles):
            columns = pl.ds(tile * 128, 128)
            products = []
            for part in range(4):
                values = []
                for which in range(2):
                    lanes = jnp.broadcast_to(pick_ref[pl.ds(which * pair_tiles + tile, 1), :] + part * 32, plane.shape)
                    values.append(jnp.take_along_axis(plane, lanes, axis=1, mode="promise_in_bounds"))
                products.append(values[0] * values[1])
            for part in range(2):
                span = pl.ds(part * rows, rows)
                even[span, columns] = (products[part] + products[part + 2]).astype(BF16)
                odd[span, columns] = (products[part] - products[part + 2]).astype(BF16)

    def horner(even, odd):
        real = dot(cos_ref[...], even[...])
        imag = dot(sin_ref[...], odd[...])
        for tile in range(pair_tiles):
            columns = pl.ds(tile * 128, 128)
            lanes = slice(tile * 128, tile * 128 + 128)
            old_re, old_im = acc_re[:, columns], acc_im[:, columns]
            acc_re[:, columns] = old_re * turn_ref[0] - old_im * turn_ref[1] + real[:, lanes]
            acc_im[:, columns] = old_re * turn_ref[1] + old_im * turn_ref[0] + imag[:, lanes]

    acc_re[...] = jnp.zeros_like(acc_re)
    acc_im[...] = jnp.zeros_like(acc_im)
    densities(side - 1, even0, odd0)

    def body(turn, _):
        x = side - 1 - 2 * turn
        densities(x - 1, even1, odd1)
        horner(even0, odd0)
        densities(jnp.maximum(x - 2, 0), even0, odd0)
        horner(even1, odd1)
        return 0

    lax.fori_loop(0, side // 2, body, 0)
    count = acc_re.shape[0]
    for tile in range(pair_tiles):
        columns = pl.ds(tile * 128, 128)
        real, imag = acc_re[:, columns], acc_im[:, columns]
        out_ref[pl.ds(0, count), columns] = (real * turn_ref[2] - imag * turn_ref[3]).astype(BF16)
        out_ref[pl.ds(count, count), columns] = (real * turn_ref[3] + imag * turn_ref[2]).astype(BF16)


def matrix_kernel(
    n, scale, rho_ref, w_hbm, out_ref, panel, w_vmem, mixed, left, pair_out, pair_in, blocks_out, blocks_in, last_out, last_in,
    w_sems, send_sems, recv_sems, left_send, left_recv, pair_sems, block_send, block_recv, last_sems,
):
    row, col = lax.axis_index("row"), lax.axis_index("col")
    waves, pairs = rho_ref.shape[0] // 2, rho_ref.shape[1]
    span = mixed.shape[1]
    per_row = span // waves
    owner_col = row // (n // 2)
    holds_left = col == owner_col
    base = lax.rem(row, n // 2) * per_row
    loads = [pltpu.make_async_copy(w_hbm.at[f, part], w_vmem.at[f, part], w_sems.at[f, part]) for f in range(2) for part in range(2)]
    for load in loads:
        load.start()
    greet(neighbours(n, 2))

    def left_copy(owner, place):
        return pltpu.make_async_remote_copy(
            src_ref=panel.at[owner],
            dst_ref=left.at[place],
            send_sem=left_send.at[place],
            recv_sem=left_recv.at[place],
            device_id={"col": 1 - col},
            device_id_type=MESH,
        )

    def multiply(owner, fresh=False):
        columns = pl.ds(pl.multiple_of(owner * waves, waves), waves)
        real, imag = panel[owner, pl.ds(0, waves)], panel[owner, pl.ds(waves, waves)]
        first = jnp.concatenate([real, imag], axis=1)
        second = jnp.concatenate([-imag, real], axis=1)

        def one(f, _):
            value = dot(w_vmem[f, 0, :, columns], first) + dot(w_vmem[f, 1, :, columns], second)
            mixed[f] = value if fresh else mixed[f] + value
            return 0

        lax.fori_loop(0, 2, one, 0)

    def on_block(owner):
        @pl.when(holds_left & (owner >= base) & (owner < base + per_row))
        def _():
            left_copy(owner, owner - base).start()

        multiply(owner)

    def before():
        panel[row] = rho_ref[...]

        @pl.when(holds_left & (row >= base) & (row < base + per_row))
        def _():
            left_copy(row, row - base).start()

        for load in loads:
            load.wait()
        multiply(row, True)

    ring = Ring(n, rho_ref, lambda owner: panel.at[owner], send_sems, recv_sems)
    ring.run(on_block, before)
    ring.drain()

    @pl.when(holds_left)
    def _():
        for place in range(per_row):
            left_copy(base + place, place).wait_send()
            left[place] = panel[base + place]

    @pl.when(jnp.logical_not(holds_left))
    def _():
        for place in range(per_row):
            left_copy(base + place, place).wait_recv()

    def elements(f):
        total = None
        for place in range(per_row):
            rows = pl.ds(place * waves, waves)
            real = mixed[f, rows, pl.ds(0, pairs)].astype(BF16)
            imag = mixed[f, rows, pl.ds(pairs, pairs)].astype(BF16)
            one = dot_tn(left[place, pl.ds(0, waves)], jnp.concatenate([real, imag], axis=1))
            two = dot_tn(left[place, pl.ds(waves, waves)], jnp.concatenate([imag, -real], axis=1))
            total = one + two if total is None else total + one + two
        return total * scale

    pair_copy = pltpu.make_async_remote_copy(
        src_ref=pair_out, dst_ref=pair_in, send_sem=pair_sems.at[0], recv_sem=pair_sems.at[1],
        device_id={"col": 1 - col}, device_id_type=MESH,
    )
    pair_out[...] = elements(1 - col).astype(BF16)
    pair_copy.start()
    value = elements(col)
    pair_copy.wait()
    value = value + pair_in[...].astype(F32)
    share = pairs // n
    for chip in range(n):
        rows = slice(chip * share, chip * share + share)
        blocks_out[chip] = jnp.concatenate([value[rows, :pairs], value[rows, pairs:]], axis=0).astype(BF16)

    def block_copy(to_row, from_row, target):
        return pltpu.make_async_remote_copy(
            src_ref=blocks_out.at[to_row],
            dst_ref=blocks_in.at[from_row],
            send_sem=block_send.at[to_row],
            recv_sem=block_recv.at[from_row],
            device_id={"row": target},
            device_id_type=MESH,
        )

    for offset in range(n - 1):
        away = n // 2 + (offset + 1) // 2 * (1 if offset % 2 else -1)
        target = lax.rem(row + away, n)
        block_copy(target, row, target).start()
    total = blocks_out[row].astype(F32)
    for offset in range(n - 1):
        away = 1 + offset // 2 if offset % 2 == 0 else n - 1 - offset // 2
        source = lax.rem(row + away, n)
        block_copy(source, source, source).wait_recv()
        total = total + blocks_in[source].astype(F32)
    for away in range(1, n):
        target = lax.rem(row + away, n)
        block_copy(target, row, target).wait_send()
    part = share // 2
    pieces = [jnp.stack([total[c * part : c * part + part], total[share + c * part : share + c * part + part]]) for c in range(2)]
    is_first = col == 0
    last_out[...] = jnp.where(is_first, pieces[1], pieces[0])
    last_copy = pltpu.make_async_remote_copy(
        src_ref=last_out, dst_ref=last_in, send_sem=last_sems.at[0], recv_sem=last_sems.at[1],
        device_id={"col": 1 - col}, device_id_type=MESH,
    )
    last_copy.start()
    out_ref[col] = jnp.where(is_first, pieces[0], pieces[1])
    last_copy.wait()
    out_ref[1 - col] = last_in[...]


VMEM = pl.BlockSpec(memory_space=pltpu.VMEM)
DMA = pltpu.SemaphoreType.DMA


def shards(n, wannier, pairs, gmap, screened):
    members, planes, cells = wannier.shape
    count = pairs.shape[0]
    tiles = count // 128
    depth = cells // 4
    quarters = wannier.reshape(members, 4, depth)
    flipped = jnp.flip(quarters[:, 2:], axis=(1, 2))
    plane = jnp.concatenate([quarters[:, :2], flipped], axis=1).transpose(2, 1, 0).reshape(depth, 4 * members).astype(BF16)

    halves = n // 2
    gathered = pl.pallas_call(
        functools.partial(planes_kernel, n),
        out_shape=jax.ShapeDtypeStruct((2 * n, depth, 4 * members), BF16),
        in_specs=[VMEM],
        out_specs=VMEM,
        scratch_shapes=[DMA((2, 2, halves)), DMA((2, 2, halves)), DMA((n,)), DMA((n,))],
        compiler_params=pltpu.CompilerParams(collective_id=0, has_side_effects=True),
        name="planes",
    )(plane)

    waves = gmap.shape[0] // (2 * n)
    start = (lax.axis_index("col") * n + lax.axis_index("row")) * waves
    cell = lax.dynamic_slice_in_dim(gmap, start, waves)
    kx, ky, kz = cell // (GX * GX), cell // GX % GX, cell % GX
    half = jnp.arange(cells // 2, dtype=jnp.int32)
    steps = (ky[:, None] * (2 * (half // GX) + 1) + kz[:, None] * (2 * (half % GX) + 1)) % (2 * GX)
    angles = steps.astype(F32) * (math.pi / GX)
    cosine, sine = jnp.cos(angles).astype(BF16), (-jnp.sin(angles)).astype(BF16)
    turn = kx.astype(F32) * (-2.0 * math.pi / GX)
    shift = ((ky + kz) % (2 * GX)).astype(F32) * (math.pi / GX)
    norm = 1.0 / math.sqrt(GX * GX * GX)
    turns = jnp.stack([jnp.cos(turn), jnp.sin(turn), jnp.cos(shift) * norm, jnp.sin(shift) * norm])
    turns = jnp.broadcast_to(turns[:, :, None], (4, waves, 128))
    picks = pairs.T.reshape(2 * tiles, 128)

    work = 2 * 2 * waves * cells // 2 * count * 2 * n
    rho = pl.pallas_call(
        functools.partial(wave_kernel, tiles),
        out_shape=jax.ShapeDtypeStruct((2 * waves, count), BF16),
        in_specs=[VMEM] * 5,
        out_specs=VMEM,
        scratch_shapes=[pltpu.VMEM((cells // 2, count), BF16)] * 4 + [pltpu.VMEM((waves, count), F32)] * 2,
        cost_estimate=pl.CostEstimate(flops=work, bytes_accessed=4 << 20, transcendentals=0),
        name="waves",
    )(gathered, picks, cosine, sine, turns)

    freqs, _, row_span, col_span = screened.shape
    share = count // n
    return pl.pallas_call(
        functools.partial(matrix_kernel, n, 1.0 / math.sqrt(gmap.shape[0])),
        out_shape=jax.ShapeDtypeStruct((freqs, 2, share // 2, count), F32),
        in_specs=[VMEM, pl.BlockSpec(memory_space=pl.ANY)],
        out_specs=VMEM,
        scratch_shapes=[
            pltpu.VMEM((n, 2 * waves, count), BF16),
            pltpu.VMEM(screened.shape, BF16),
            pltpu.VMEM((freqs, row_span, 2 * count), F32),
            pltpu.VMEM((row_span // waves, 2 * waves, count), BF16),
            pltpu.VMEM((count, 2 * count), BF16),
            pltpu.VMEM((count, 2 * count), BF16),
            pltpu.VMEM((n, 2 * share, count), BF16),
            pltpu.VMEM((n, 2 * share, count), BF16),
            pltpu.VMEM((2, share // 2, count), F32),
            pltpu.VMEM((2, share // 2, count), F32),
            DMA((2, 2)),
            DMA((2, 2, halves)),
            DMA((2, 2, halves)),
            DMA((row_span // waves,)),
            DMA((row_span // waves,)),
            DMA((2,)),
            DMA((n,)),
            DMA((n,)),
            DMA((2,)),
        ],
        compiler_params=pltpu.CompilerParams(collective_id=1, has_side_effects=True, vmem_limit_bytes=60 << 20),
        name="matrix",
    )(rho, screened)


def solution(mesh):
    return jax.shard_map(
        functools.partial(shards, mesh.shape["row"]),
        mesh=mesh,
        in_specs=(P("kpt", ("row", "col"), None), P(), P(), P("kpt", None, "row", "col")),
        out_specs=P(None, None, ("kpt", "row", "col"), None),
        check_vma=False,
    )
```

time: 504 us -> 183 us (0.36); the launches traced: 495 us -> 183 us
  local copies, waits for them, and re-layouts: 195 us -> 5.14 us
  Pallas kernels: 0 us -> 172 us
  waiting for transfers between devices: 115 us -> 0 us
  blocking collectives: 74.4 us -> 0 us
  matrix products: 57.8 us -> 0 us
  starting transfers between devices: 23.2 us -> 0 us
  between operations: 14.2 us -> 0.08 us
  other arithmetic: 16 us -> 5.34 us
    pallas_call x0 -> x3, Pallas kernels: none -> 172 us  [the longest x1 105 us: shards(): pl.pallas_call(functools.partial(matrix_kernel, n, 1.0 / math.sqrt(gmap.s...]
    all_to_all x2 -> x0, blocking collectives: 74.4 us -> none  [the longest x1 70 us: sum_at_owner(): lax.all_to_all(pieces, axis, split_axis=0, concat_axis=0, tiled=True)]
    all_gather x1 -> x0, waiting for transfers between devices: 70.5 us -> none  [shards(): right_panel = lax.all_gather(halves, 'row', axis=1, tiled=True)]
    gather x2 -> x0, local copies, waits for them, and re-layouts: 67 us -> none  [the longest x1 33.5 us: shards(): jnp.take(imag_part.reshape(owned, -1), gmap, axis=1) * norm_factor]
    dot_general x20 -> x0, matrix products: 57.8 us -> none  [the longest x1 6.87 us: right_columns(): jnp.einsum('fgh,bh->fgb', w_imag, segment[0], preferred_element_type=jnp....]
    all_to_all x1 -> x0, waiting for transfers between devices: 44.3 us -> none  [shards(): lax.all_to_all(density.astype(jnp.bfloat16), ('row', 'col'), split_axis=0...]
    reshape x6 -> x2, local copies, waits for them, and re-layouts: 40 us -> 1.31 us  [the longest x1 1.28 us: shards(): picks = pairs.T.reshape(2 * tiles, 128)]
    another operation x1 -> x0, local copies, waits for them, and re-layouts: 35.4 us -> none  [shards(): rho = jnp.stack([rho_real, rho_imag], axis=0).astype(jnp.bfloat16)]
  transfers between devices with their start and end apart: 3 -> 0, of which waited for: 2 -> 0; matrix products, arithmetic and copies ran while one was open for 5% -> 0% of each run, Pallas kernels for 0% -> 0%
where the time goes in v1:
time: 183 us
  Pallas kernels  172 us (94%)
  other arithmetic  5.34 us (3%)
  local copies, waits for them, and re-layouts  5.14 us (3%)
    pallas_call x1, Pallas kernels, shards(): pl.pallas_call(functools.partial(matrix_kernel, n, 1.0 / math.sqrt(gmap.s...  105 us
    pallas_call x1, Pallas kernels, shards(): pl.pallas_call(functools.partial(planes_kernel, n), out_shape=jax.ShapeDt...  43.7 us
    pallas_call x1, Pallas kernels, shards(): pl.pallas_call(functools.partial(wave_kernel, tiles), out_shape=jax.Shape...  23.4 us

profile of v1, /device:TPU:69, one launch (start us, length us, event | category | flops | bytes accessed | tf_op | source)
XLA Modules:
  0.0 182.9 jit_solution(967584147866517239)
XLA Ops:
  0.0 1.3 reshape.38.pick_ref
  1.3 0.8 fusion.18
  2.2 1.2 reduce
  3.5 0.1 fusion.20
  3.5 0.4 rev.4
  4.0 0.1 maximum_bitcast_fusion
  4.1 0.7 copy.11.own_ref
  4.8 1.0 broadcast_in_dim.2.turn_ref
  5.8 3.2 %negate_convert_fusion = (bf16[256,512]{1,0:T(8,128)(2,1)}, bf16[256,512]{1,0:T(8,128)(2,1)}) fusion(s32[512]{0:T(512)S(1)} %get-tuple-element.20, s32[256]{0:T(256)S(1)} %get-tuple-element.15, s32[512]{0:T(512)S(1)} %get-tuple-element.19, s32[256]{0:T(256)S(1)} %get-tuple-element.16), kind=kLoop, calls=%fused_computation.6 | loop fusion | flops 2490368 | bytes 530432 | tf_op jit(solution)/shard_map/convert_element_type | solution.py:361
  9.0 43.7 %planes.1.w_ref = bf16[32,256,128]{2,1,0:T(8,128)(2,1)} custom-call(bf16[256,128]{1,0:T(8,128)(2,1)} %copy.11.own_ref), custom_call_target="tpu_custom_call" | custom-call | tf_op jit(solution)/shard_map/planes/pallas_call | solution.py:344
  52.7 23.4 %waves.1.rho_ref = bf16[512,384]{1,0:T(8,128)(2,1)} custom-call(bf16[32,256,128]{2,1,0:T(8,128)(2,1)} %planes.1.w_ref, s32[6,128]{1,0:T(8,128)} %reshape.38.pick_ref, bf16[256,512]{1,0:T(8,128)(2,1)} %get-tuple-element.18.cos_ref, bf16[256,512]{1,0:T(8,128)(2,1)} %get-tuple-element.17.sin_ref, f32[4,256,128]{2,1,0:T(8,128)} %broadcast_in_dim.2.turn_ref), custom_call_target="tpu_custom_call" | custom-call | flops 6442450944 | bytes 4194304 | tf_op jit(solution)/shard_map/waves/pallas_call | solution.py:370
  76.0 105.3 %matrix.1 = f32[2,2,12,384]{3,2,1,0:T(8,128)} custom-call(bf16[512,384]{1,0:T(8,128)(2,1)} %waves.1.rho_ref, bf16[2,2,512,4096]{3,2,1,0:T(8,128)(2,1)} %w_hbm.1), custom_call_target="tpu_custom_call" | custom-call | tf_op jit(solution)/shard_map/matrix/pallas_call | solution.py:382
  181.3 1.6 copy.12
  (6 shorter events, 0.1 us)

commit v2 on v1

--- a/solution.py
+++ b/solution.py
@@ -105,92 +105,190 @@
     return [{"row": right}, {"row": left}, {"col": 1 - col}]
 
 
-def planes_kernel(n, own_ref, out_ref, send_sems, recv_sems, pair_send, pair_recv):
+def pick_lanes(values, lanes):
+    numbers = lax.GatherDimensionNumbers(
+        offset_dims=(), collapsed_slice_dims=(1,), start_index_map=(1,), operand_batching_dims=(0,), start_indices_batching_dims=(0,)
+    )
+    return lax.gather(values, lanes[:, :, None], numbers, (1, 1), mode=lax.GatherScatterMode.PROMISE_IN_BOUNDS)
+
+
+def wave_kernel(
+    n, own_ref, pick_ref, cell_ref, out_ref, planes, cosine, sine, turn, power, even0, odd0, even1, odd1, acc_re, acc_im,
+    send_sems, recv_sems, pair_send, pair_recv,
+):
     row, col = lax.axis_index("row"), lax.axis_index("col")
+    depth = own_ref.shape[0]
+    waves, pairs = acc_re.shape
+    tiles = pairs // 128
+    piece = 64
     greet(neighbours(n, 2))
 
-    def slot(owner):
-        return out_ref.at[owner * 2 + col]
+    def slot(owner, which):
+        return planes.at[owner * 2 + which]
 
     def pair_copy(source, owner, to_col):
         return pltpu.make_async_remote_copy(
             src_ref=source,
-            dst_ref=out_ref.at[owner * 2 + to_col],
+            dst_ref=slot(owner, to_col),
             send_sem=pair_send.at[owner],
             recv_sem=pair_recv.at[owner],
             device_id={"col": 1 - col},
             device_id_type=MESH,
         )
 
-    ring = Ring(n, own_ref, slot, send_sems, recv_sems)
-
-    def before():
-        pair_copy(own_ref, row, col).start()
-        out_ref[row * 2 + col] = own_ref[...]
-
-    def on_block(owner):
-        pair_copy(slot(owner), owner, col).start()
-
-    ring.run(on_block, before)
-    ring.drain()
-
-    def finish(owner, _):
-        pair_copy(slot(owner), owner, col).wait_send()
-        pair_copy(slot(owner), owner, 1 - col).wait_recv()
-        return 0
-
-    lax.fori_loop(0, n, finish, 0)
-
-
-def wave_kernel(pair_tiles, w_ref, pick_ref, cos_ref, sin_ref, turn_ref, out_ref, even0, odd0, even1, odd1, acc_re, acc_im):
-    side = w_ref.shape[0]
-    rows = w_ref.shape[1]
-
-    def densities(x, even, odd):
-        plane = w_ref[x].astype(F32)
-        for tile in range(pair_tiles):
-            columns = pl.ds(tile * 128, 128)
-            products = []
-            for part in range(4):
-                values = []
-                for which in range(2):
-                    lanes = jnp.broadcast_to(pick_ref[pl.ds(which * pair_tiles + tile, 1), :] + part * 32, plane.shape)
-                    values.append(jnp.take_along_axis(plane, lanes, axis=1, mode="promise_in_bounds"))
-                products.append(values[0] * values[1])
-            for part in range(2):
-                span = pl.ds(part * rows, rows)
-                even[span, columns] = (products[part] + products[part + 2]).astype(BF16)
-                odd[span, columns] = (products[part] - products[part + 2]).astype(BF16)
-
-    def horner(even, odd):
-        real = dot(cos_ref[...], even[...])
-        imag = dot(sin_ref[...], odd[...])
-        for tile in range(pair_tiles):
-            columns = pl.ds(tile * 128, 128)
-            lanes = slice(tile * 128, tile * 128 + 128)
-            old_re, old_im = acc_re[:, columns], acc_im[:, columns]
-            acc_re[:, columns] = old_re * turn_ref[0] - old_im * turn_ref[1] + real[:, lanes]
-            acc_im[:, columns] = old_re * turn_ref[1] + old_im * turn_ref[0] + imag[:, lanes]
-
+    def fold(owner, tile, even, odd):
+        for which in range(2):
+            columns = pl.ds(pl.multiple_of(tile * 256 + which * 128, 128), 128)
+            for begin in range(0, depth, piece):
+                plane = planes[owner * 2 + which, pl.ds(begin, piece)].astype(F32)
+                for part in range(2):
+                    values = []
+                    for quarter in (part, part + 2):
+                        for side in range(2):
+                            lanes = pick_ref[pl.ds(side * tiles + tile, 1), :] + quarter * 32
+                            values.append(pick_lanes(plane, jnp.broadcast_to(lanes, plane.shape)))
+                    one, two = values[0] * values[1], values[2] * values[3]
+                    span = pl.ds(part * depth + begin, piece)
+                    even[span, columns] = (one + two).astype(BF16)
+                    odd[span, columns] = (one - two).astype(BF16)
+
+    def gather(tile, even, odd, sign):
+        columns = pl.ds(pl.multiple_of(tile * 128, 128), 128)
+        block = pl.ds(pl.multiple_of(tile * 256, 256), 256)
+        real = dot(cosine[...], even[:, block])
+        imag = dot(sine[...], odd[:, block])
+        p_re, p_im = power[0], power[1] * sign
+        q_re, q_im = p_re * turn[0] - p_im * turn[1], p_re * turn[1] + p_im * turn[0]
+        acc_re[:, columns] += p_re * real[:, :128] - p_im * imag[:, :128] + (q_re * real[:, 128:] - q_im * imag[:, 128:])
+        acc_im[:, columns] += p_re * imag[:, :128] + p_im * real[:, :128] + (q_re * imag[:, 128:] + q_im * real[:, 128:])
+
+    def tables():
+        lane = lax.broadcasted_iota(jnp.int32, (8, 128), 1)
+        angle = (lane & (2 * GX - 1)).astype(F32) * (math.pi / GX)
+        cos_lanes, sin_lanes = jnp.cos(angle), jnp.sin(angle)
+        copies = waves // 8
+
+        def look(steps):
+            at = steps & (2 * GX - 1)
+            return (
+                pick_lanes(jnp.concatenate([cos_lanes] * copies, axis=0), at),
+                pick_lanes(jnp.concatenate([sin_lanes] * copies, axis=0), at),
+            )
+
+        bits = GX.bit_length() - 1
+        cell = cell_ref[...]
+        kx, ky, kz = cell >> (2 * bits), (cell >> bits) & (GX - 1), cell & (GX - 1)
+
+        def fill(index, _):
+            begin = pl.multiple_of(index * 128, 128)
+            spot = lax.broadcasted_iota(jnp.int32, cell.shape, 1) + begin
+            real, imag = look(ky * (2 * (spot >> bits) + 1) + kz * (2 * (spot & (GX - 1)) + 1))
+            cosine[:, pl.ds(begin, 128)] = real.astype(BF16)
+            sine[:, pl.ds(begin, 128)] = (-imag).astype(BF16)
+            return 0
+
+        lax.fori_loop(0, 2 * depth // 128, fill, 0)
+        turn[0], turn[1] = look(kx * -2)
+        turn[2], turn[3] = look(kx * -4)
+        norm = 1.0 / math.sqrt(GX * GX * GX)
+        real, imag = look(ky + kz - kx * 4 * row)
+        turn[4], turn[5] = real * norm, imag * norm
+        power[0] = jnp.ones(cell.shape, F32)
+        power[1] = jnp.zeros(cell.shape, F32)
+
+    def advance():
+        p_re, p_im = power[0], power[1]
+        power[0] = p_re * turn[2] - p_im * turn[3]
+        power[1] = p_re * turn[3] + p_im * turn[2]
+
+    ring = Ring(n, own_ref, lambda owner: slot(owner, col), send_sems, recv_sems)
+    half = n // 2
+
+    def arrive(step):
+        for chunk in range(2):
+            for way in range(2):
+                if way == chunk:
+                    ring.copy(way, chunk, step - 1, False, True).wait_recv()
+
+                    @pl.when(step < half)
+                    def _():
+                        ring.copy(way, chunk, step, False).start()
+                else:
+                    @pl.when(step < half)
+                    def _():
+                        ring.copy(way, chunk, step - 1, False, True).wait_recv()
+
+                    @pl.when(step < half - 1)
+                    def _():
+                        ring.copy(way, chunk, step, False).start()
+        ahead, behind = ring.owner(1, step), ring.owner(0, step)
+        pair_copy(slot(ahead, col), ahead, col).start()
+
+        @pl.when(step < half)
+        def _():
+            pair_copy(slot(behind, col), behind, col).start()
+
+    def paired(owner):
+        pair_copy(own_ref, owner, 1 - col).wait_recv()
+
+    def each_tile(work):
+        def one(tile, _):
+            work(tile)
+            return 0
+
+        lax.fori_loop(0, tiles, one, 0)
+
+    def first_half(owner):
+        def work(tile):
+            gather(tile, even1, odd1, -1.0)
+            fold(owner, tile, even0, odd0)
+
+        each_tile(work)
+        advance()
+
+    for way in range(2):
+        for chunk in range(2):
+            ring.copy(way, chunk, 0, True).start()
+    pair_copy(own_ref, row, col).start()
+    planes[row * 2 + col] = own_ref[...]
     acc_re[...] = jnp.zeros_like(acc_re)
     acc_im[...] = jnp.zeros_like(acc_im)
-    densities(side - 1, even0, odd0)
-
-    def body(turn, _):
-        x = side - 1 - 2 * turn
-        densities(x - 1, even1, odd1)
-        horner(even0, odd0)
-        densities(jnp.maximum(x - 2, 0), even0, odd0)
-        horner(even1, odd1)
+    tables()
+    arrive(1)
+    paired(row)
+    each_tile(lambda tile: fold(row, tile, even1, odd1))
+
+    def body(step, _):
+        arrive(step)
+        ahead, behind = ring.owner(1, step - 1), ring.owner(0, step - 1)
+        paired(ahead)
+        paired(behind)
+        first_half(ahead)
+
+        def work(tile):
+            gather(tile, even0, odd0, 1.0)
+            fold(behind, tile, even1, odd1)
+
+        each_tile(work)
         return 0
 
-    lax.fori_loop(0, side // 2, body, 0)
-    count = acc_re.shape[0]
-    for tile in range(pair_tiles):
+    lax.fori_loop(2, half + 1, body, 0)
+    across = ring.owner(0, half)
+    paired(across)
+    first_half(across)
+    each_tile(lambda tile: gather(tile, even0, odd0, 1.0))
+    for tile in range(tiles):
         columns = pl.ds(tile * 128, 128)
         real, imag = acc_re[:, columns], acc_im[:, columns]
-        out_ref[pl.ds(0, count), columns] = (real * turn_ref[2] - imag * turn_ref[3]).astype(BF16)
-        out_ref[pl.ds(count, count), columns] = (real * turn_ref[3] + imag * turn_ref[2]).astype(BF16)
+        out_ref[pl.ds(0, waves), columns] = (real * turn[4] - imag * turn[5]).astype(BF16)
+        out_ref[pl.ds(waves, waves), columns] = (real * turn[5] + imag * turn[4]).astype(BF16)
+    ring.drain()
+
+    def finish(owner, _):
+        pair_copy(own_ref, owner, col).wait_send()
+        return 0
+
+    lax.fori_loop(0, n, finish, 0)
 
 
 def matrix_kernel(
@@ -341,41 +439,28 @@
     plane = jnp.concatenate([quarters[:, :2], flipped], axis=1).transpose(2, 1, 0).reshape(depth, 4 * members).astype(BF16)
 
     halves = n // 2
-    gathered = pl.pallas_call(
-        functools.partial(planes_kernel, n),
-        out_shape=jax.ShapeDtypeStruct((2 * n, depth, 4 * members), BF16),
-        in_specs=[VMEM],
-        out_specs=VMEM,
-        scratch_shapes=[DMA((2, 2, halves)), DMA((2, 2, halves)), DMA((n,)), DMA((n,))],
-        compiler_params=pltpu.CompilerParams(collective_id=0, has_side_effects=True),
-        name="planes",
-    )(plane)
-
     waves = gmap.shape[0] // (2 * n)
     start = (lax.axis_index("col") * n + lax.axis_index("row")) * waves
-    cell = lax.dynamic_slice_in_dim(gmap, start, waves)
-    kx, ky, kz = cell // (GX * GX), cell // GX % GX, cell % GX
-    half = jnp.arange(cells // 2, dtype=jnp.int32)
-    steps = (ky[:, None] * (2 * (half // GX) + 1) + kz[:, None] * (2 * (half % GX) + 1)) % (2 * GX)
-    angles = steps.astype(F32) * (math.pi / GX)
-    cosine, sine = jnp.cos(angles).astype(BF16), (-jnp.sin(angles)).astype(BF16)
-    turn = kx.astype(F32) * (-2.0 * math.pi / GX)
-    shift = ((ky + kz) % (2 * GX)).astype(F32) * (math.pi / GX)
-    norm = 1.0 / math.sqrt(GX * GX * GX)
-    turns = jnp.stack([jnp.cos(turn), jnp.sin(turn), jnp.cos(shift) * norm, jnp.sin(shift) * norm])
-    turns = jnp.broadcast_to(turns[:, :, None], (4, waves, 128))
+    cell = jnp.broadcast_to(lax.dynamic_slice_in_dim(gmap, start, waves)[:, None], (waves, 128))
     picks = pairs.T.reshape(2 * tiles, 128)
-
-    work = 2 * 2 * waves * cells // 2 * count * 2 * n
     rho = pl.pallas_call(
-        functools.partial(wave_kernel, tiles),
+        functools.partial(wave_kernel, n),
         out_shape=jax.ShapeDtypeStruct((2 * waves, count), BF16),
-        in_specs=[VMEM] * 5,
+        in_specs=[VMEM] * 3,
         out_specs=VMEM,
-        scratch_shapes=[pltpu.VMEM((cells // 2, count), BF16)] * 4 + [pltpu.VMEM((waves, count), F32)] * 2,
-        cost_estimate=pl.CostEstimate(flops=work, bytes_accessed=4 << 20, transcendentals=0),
+        scratch_shapes=[
+            pltpu.VMEM((2 * n, depth, 4 * members), BF16),
+            pltpu.VMEM((waves, cells // 2), BF16),
+            pltpu.VMEM((waves, cells // 2), BF16),
+            pltpu.VMEM((6, waves, 128), F32),
+            pltpu.VMEM((2, waves, 128), F32),
+        ]
+        + [pltpu.VMEM((cells // 2, 2 * count), BF16)] * 4
+        + [pltpu.VMEM((waves, count), F32)] * 2
+        + [DMA((2, 2, halves)), DMA((2, 2, halves)), DMA((n,)), DMA((n,))],
+        compiler_params=pltpu.CompilerParams(collective_id=0, has_side_effects=True),
         name="waves",
-    )(gathered, picks, cosine, sine, turns)
+    )(plane, picks, cell)
 
     freqs, _, row_span, col_span = screened.shape
     share = count // n

time: 183 us -> 163 us (0.89)
  Pallas kernels: 172 us -> 156 us
  other arithmetic: 5.34 us -> 1.3 us
    pallas_call x2 -> x1, Pallas kernels: 67.1 us -> 49.5 us  [shards(): pl.pallas_call(functools.partial(wave_kernel, n), out_shape=jax.ShapeDtyp...]
    convert_element_type x1 -> x0, other arithmetic: 3.16 us -> none  [shards(): (-jnp.sin(angles)).astype(BF16)]
where the time goes in v2:
time: 163 us
  Pallas kernels  156 us (96%)
  local copies, waits for them, and re-layouts  5.62 us (3%)
    pallas_call x1, Pallas kernels, shards(): pl.pallas_call(functools.partial(matrix_kernel, n, 1.0 / math.sqrt(gmap.s...  107 us
    pallas_call x1, Pallas kernels, shards(): pl.pallas_call(functools.partial(wave_kernel, n), out_shape=jax.ShapeDtyp...  49.5 us

profile of v2, /device:TPU:69, one launch (start us, length us, event | category | flops | bytes accessed | tf_op | source)
XLA Modules:
  0.0 163.1 jit_solution(8387287947484518353)
XLA Ops:
  0.0 0.8 dynamic_slice.3
  0.8 1.3 reshape.10.pick_ref
  2.0 1.2 reduce
  3.3 0.1 fusion
  3.4 0.4 rev.4
  3.8 0.1 maximum_bitcast_fusion
  3.9 0.7 copy.11.own_ref
  4.6 0.8 broadcast_in_dim.2.cell_ref
  5.4 49.5 %waves.1.rho_ref = bf16[512,384]{1,0:T(8,128)(2,1)} custom-call(bf16[256,128]{1,0:T(8,128)(2,1)} %copy.11.own_ref, s32[6,128]{1,0:T(8,128)} %reshape.10.pick_ref, s32[256,128]{1,0:T(8,128)} %broadcast_in_dim.2.cell_ref), custom_call_target="tpu_custom_call" | custom-call | tf_op jit(solution)/shard_map/waves/pallas_call | solution.py:446
  54.9 106.5 %matrix.1 = f32[2,2,12,384]{3,2,1,0:T(8,128)} custom-call(bf16[512,384]{1,0:T(8,128)(2,1)} %waves.1.rho_ref, bf16[2,2,512,4096]{3,2,1,0:T(8,128)(2,1)} %w_hbm.1), custom_call_target="tpu_custom_call" | custom-call | tf_op jit(solution)/shard_map/matrix/pallas_call | solution.py:467
  161.5 1.6 copy.12
  (2 shorter events, 0.0 us)

commit v3 on v2

--- a/solution.py
+++ b/solution.py
@@ -22,10 +22,12 @@
     return lax.dot_general(a, b, (((0,), (0,)), ((), ())), preferred_element_type=F32)
 
 
-def greet(targets):
+def greet(targets, between=None):
     barrier = pltpu.get_barrier_semaphore()
     for target in targets:
         pl.semaphore_signal(barrier, inc=1, device_id=target, device_id_type=MESH)
+    if between is not None:
+        between()
     pl.semaphore_wait(barrier, len(targets))
 
 
@@ -113,7 +115,7 @@
 
 
 def wave_kernel(
-    n, own_ref, pick_ref, cell_ref, out_ref, planes, cosine, sine, turn, power, even0, odd0, even1, odd1, acc_re, acc_im,
+    n, wannier_ref, pick_ref, gmap_ref, out_ref, own_ref, cell_ref, planes, cosine, sine, turn, power, even0, odd0, even1, odd1, acc_re, acc_im,
     send_sems, recv_sems, pair_send, pair_recv,
 ):
     row, col = lax.axis_index("row"), lax.axis_index("col")
@@ -121,7 +123,20 @@
     waves, pairs = acc_re.shape
     tiles = pairs // 128
     piece = 64
-    greet(neighbours(n, 2))
+
+    def prepare():
+        values = wannier_ref[:, 0, :]
+        back = 127 - lax.broadcasted_iota(jnp.int32, (values.shape[0], 128), 1)
+        parts = [values[:, :depth], values[:, depth : 2 * depth]]
+        for quarter in (3, 2):
+            tail = [pick_lanes(values[:, quarter * depth + lane : quarter * depth + lane + 128], back) for lane in range(0, depth, 128)]
+            parts.append(jnp.concatenate(tail[::-1], axis=1))
+        own_ref[...] = jnp.concatenate(parts, axis=0).T.astype(BF16)
+        for begin in range(0, waves, 128):
+            line = gmap_ref[pl.ds((col * n + row) * (waves // 128) + begin // 128, 1), :].astype(F32)
+            cell_ref[pl.ds(begin, 128)] = jnp.broadcast_to(line, (128, 128)).T.astype(jnp.int32)
+
+    greet(neighbours(n, 2), prepare)
 
     def slot(owner, which):
         return planes.at[owner * 2 + which]
@@ -145,7 +160,7 @@
                     values = []
                     for quarter in (part, part + 2):
                         for side in range(2):
-                            lanes = pick_ref[pl.ds(side * tiles + tile, 1), :] + quarter * 32
+                            lanes = pick_ref[pl.ds(side, 1), pl.ds(pl.multiple_of(tile * 128, 128), 128)] + quarter * 32
                             values.append(pick_lanes(plane, jnp.broadcast_to(lanes, plane.shape)))
                     one, two = values[0] * values[1], values[2] * values[3]
                     span = pl.ds(part * depth + begin, piece)
@@ -158,9 +173,17 @@
         real = dot(cosine[...], even[:, block])
         imag = dot(sine[...], odd[:, block])
         p_re, p_im = power[0], power[1] * sign
-        q_re, q_im = p_re * turn[0] - p_im * turn[1], p_re * turn[1] + p_im * turn[0]
+        at = 2 if sign > 0 else 4
+        q_re, q_im = power[at], power[at + 1]
         acc_re[:, columns] += p_re * real[:, :128] - p_im * imag[:, :128] + (q_re * real[:, 128:] - q_im * imag[:, 128:])
         acc_im[:, columns] += p_re * imag[:, :128] + p_im * real[:, :128] + (q_re * imag[:, 128:] + q_im * real[:, 128:])
+
+    def set_power(p_re, p_im):
+        power[0], power[1] = p_re, p_im
+        one, two = p_re * turn[0], p_im * turn[1]
+        three, four = p_re * turn[1], p_im * turn[0]
+        power[2], power[3] = one - two, three + four
+        power[4], power[5] = one + two, three - four
 
     def tables():
         lane = lax.broadcasted_iota(jnp.int32, (8, 128), 1)
@@ -193,13 +216,11 @@
         norm = 1.0 / math.sqrt(GX * GX * GX)
         real, imag = look(ky + kz - kx * 4 * row)
         turn[4], turn[5] = real * norm, imag * norm
-        power[0] = jnp.ones(cell.shape, F32)
-        power[1] = jnp.zeros(cell.shape, F32)
+        set_power(jnp.ones(cell.shape, F32), jnp.zeros(cell.shape, F32))
 
     def advance():
         p_re, p_im = power[0], power[1]
-        power[0] = p_re * turn[2] - p_im * turn[3]
-        power[1] = p_re * turn[3] + p_im * turn[2]
+        set_power(p_re * turn[2] - p_im * turn[3], p_re * turn[3] + p_im * turn[2])
 
     ring = Ring(n, own_ref, lambda owner: slot(owner, col), send_sems, recv_sems)
     half = n // 2
@@ -292,8 +313,9 @@
 
 
 def matrix_kernel(
-    n, scale, rho_ref, w_hbm, out_ref, panel, w_vmem, mixed, left, pair_out, pair_in, blocks_out, blocks_in, last_out, last_in,
-    w_sems, send_sems, recv_sems, left_send, left_recv, pair_sems, block_send, block_recv, last_sems,
+    n, scale, rho_ref, w_hbm, out_ref, panel, w_vmem, mixed, left, pair_out, pair_in, own_sums, near_out, near_in,
+    far_out, far_in, last_out, last_in, w_sems, send_sems, recv_sems, left_send, left_recv, pair_sems, near_send, near_recv,
+    far_send, far_recv, last_sems,
 ):
     row, col = lax.axis_index("row"), lax.axis_index("col")
     waves, pairs = rho_ref.shape[0] // 2, rho_ref.shape[1]
@@ -384,33 +406,56 @@
     pair_copy.wait()
     value = value + pair_in[...].astype(F32)
     share = pairs // n
+    odd = lax.rem(row, 2)
     for chip in range(n):
         rows = slice(chip * share, chip * share + share)
-        blocks_out[chip] = jnp.concatenate([value[rows, :pairs], value[rows, pairs:]], axis=0).astype(BF16)
-
-    def block_copy(to_row, from_row, target):
+        block = jnp.concatenate([value[rows, :pairs], value[rows, pairs:]], axis=0)
+        place = (chip % 2, chip // 2 % 2, chip // 4)
+        own_sums[place] = block
+        near_out[place] = block.astype(BF16)
+
+    def near_copy(way):
+        step = lax.rem(odd + way, 2) * -2 + 1
         return pltpu.make_async_remote_copy(
-            src_ref=blocks_out.at[to_row],
-            dst_ref=blocks_in.at[from_row],
-            send_sem=block_send.at[to_row],
-            recv_sem=block_recv.at[from_row],
+            src_ref=near_out.at[1 - odd, way],
+            dst_ref=near_in.at[way],
+            send_sem=near_send.at[way],
+            recv_sem=near_recv.at[way],
+            device_id={"row": lax.rem(row + step + n, n)},
+            device_id_type=MESH,
+        )
+
+    def far_copy(to_row, from_row, target):
+        return pltpu.make_async_remote_copy(
+            src_ref=far_out.at[lax.rem(to_row // 2, 2), to_row // 4],
+            dst_ref=far_in.at[from_row // 2],
+            send_sem=far_send.at[to_row // 2],
+            recv_sem=far_recv.at[from_row // 2],
             device_id={"row": target},
             device_id_type=MESH,
         )
 
-    for offset in range(n - 1):
-        away = n // 2 + (offset + 1) // 2 * (1 if offset % 2 else -1)
-        target = lax.rem(row + away, n)
-        block_copy(target, row, target).start()
-    total = blocks_out[row].astype(F32)
-    for offset in range(n - 1):
-        away = 1 + offset // 2 if offset % 2 == 0 else n - 1 - offset // 2
-        source = lax.rem(row + away, n)
-        block_copy(source, source, source).wait_recv()
-        total = total + blocks_in[source].astype(F32)
-    for away in range(1, n):
-        target = lax.rem(row + away, n)
-        block_copy(target, row, target).wait_send()
+    for way in range(2):
+        near_copy(way).start()
+    for way in range(2):
+        near_copy(way).wait()
+        both = own_sums[odd, way] + near_in[way].astype(F32)
+        own_sums[odd, way] = both
+        far_out[way] = both.astype(BF16)
+    chips = n // 2
+    for offset in range(chips - 1):
+        away = chips // 2 + (offset + 1) // 2 * (1 if offset % 2 else -1)
+        target = lax.rem(row + 2 * away, n)
+        far_copy(target, row, target).start()
+    total = own_sums[odd, lax.rem(row // 2, 2), row // 4]
+    for offset in range(chips - 1):
+        away = 1 + offset // 2 if offset % 2 == 0 else chips - 1 - offset // 2
+        source = lax.rem(row + 2 * away, n)
+        far_copy(source, source, source).wait_recv()
+        total = total + far_in[source // 2].astype(F32)
+    for away in range(1, chips):
+        target = lax.rem(row + 2 * away, n)
+        far_copy(target, row, target).wait_send()
     part = share // 2
     pieces = [jnp.stack([total[c * part : c * part + part], total[share + c * part : share + c * part + part]]) for c in range(2)]
     is_first = col == 0
@@ -432,35 +477,29 @@
 def shards(n, wannier, pairs, gmap, screened):
     members, planes, cells = wannier.shape
     count = pairs.shape[0]
-    tiles = count // 128
     depth = cells // 4
-    quarters = wannier.reshape(members, 4, depth)
-    flipped = jnp.flip(quarters[:, 2:], axis=(1, 2))
-    plane = jnp.concatenate([quarters[:, :2], flipped], axis=1).transpose(2, 1, 0).reshape(depth, 4 * members).astype(BF16)
-
     halves = n // 2
     waves = gmap.shape[0] // (2 * n)
-    start = (lax.axis_index("col") * n + lax.axis_index("row")) * waves
-    cell = jnp.broadcast_to(lax.dynamic_slice_in_dim(gmap, start, waves)[:, None], (waves, 128))
-    picks = pairs.T.reshape(2 * tiles, 128)
     rho = pl.pallas_call(
         functools.partial(wave_kernel, n),
         out_shape=jax.ShapeDtypeStruct((2 * waves, count), BF16),
         in_specs=[VMEM] * 3,
         out_specs=VMEM,
         scratch_shapes=[
+            pltpu.VMEM((depth, 4 * members), BF16),
+            pltpu.VMEM((waves, 128), jnp.int32),
             pltpu.VMEM((2 * n, depth, 4 * members), BF16),
             pltpu.VMEM((waves, cells // 2), BF16),
             pltpu.VMEM((waves, cells // 2), BF16),
             pltpu.VMEM((6, waves, 128), F32),
-            pltpu.VMEM((2, waves, 128), F32),
+            pltpu.VMEM((6, waves, 128), F32),
         ]
         + [pltpu.VMEM((cells // 2, 2 * count), BF16)] * 4
         + [pltpu.VMEM((waves, count), F32)] * 2
         + [DMA((2, 2, halves)), DMA((2, 2, halves)), DMA((n,)), DMA((n,))],
         compiler_params=pltpu.CompilerParams(collective_id=0, has_side_effects=True),
         name="waves",
-    )(plane, picks, cell)
+    )(wannier, pairs.T, gmap.reshape(-1, 128))
 
     freqs, _, row_span, col_span = screened.shape
     share = count // n
@@ -476,8 +515,11 @@
             pltpu.VMEM((row_span // waves, 2 * waves, count), BF16),
             pltpu.VMEM((count, 2 * count), BF16),
             pltpu.VMEM((count, 2 * count), BF16),
-            pltpu.VMEM((n, 2 * share, count), BF16),
-            pltpu.VMEM((n, 2 * share, count), BF16),
+            pltpu.VMEM((2, 2, n // 4, 2 * share, count), F32),
+            pltpu.VMEM((2, 2, n // 4, 2 * share, count), BF16),
+            pltpu.VMEM((2, n // 4, 2 * share, count), BF16),
+            pltpu.VMEM((2, n // 4, 2 * share, count), BF16),
+            pltpu.VMEM((n // 2, 2 * share, count), BF16),
             pltpu.VMEM((2, share // 2, count), F32),
             pltpu.VMEM((2, share // 2, count), F32),
             DMA((2, 2)),
@@ -486,8 +528,10 @@
             DMA((row_span // waves,)),
             DMA((row_span // waves,)),
             DMA((2,)),
-            DMA((n,)),
-            DMA((n,)),
+            DMA((2,)),
+            DMA((2,)),
+            DMA((halves,)),
+            DMA((halves,)),
             DMA((2,)),
         ],
         compiler_params=pltpu.CompilerParams(collective_id=1, has_side_effects=True, vmem_limit_bytes=60 << 20),

time: 163 us -> 153 us (0.939)
  Pallas kernels: 156 us -> 151 us
  local copies, waits for them, and re-layouts: 5.62 us -> 1.56 us
    pallas_call x1, Pallas kernels: 107 us -> 101 us  [shards(): pl.pallas_call(functools.partial(matrix_kernel, n, 1.0 / math.sqrt(gmap.s...]
where the time goes in v3:
time: 153 us
  Pallas kernels  151 us (99%)
  local copies, waits for them, and re-layouts  1.56 us (1%)
    pallas_call x1, Pallas kernels, shards(): pl.pallas_call(functools.partial(matrix_kernel, n, 1.0 / math.sqrt(gmap.s...  101 us
    pallas_call x1, Pallas kernels, shards(): pl.pallas_call(functools.partial(wave_kernel, n), out_shape=jax.ShapeDtyp...  50 us

profile of v3, /device:TPU:69, one launch (start us, length us, event | category | flops | bytes accessed | tf_op | source)
XLA Modules:
  0.0 152.8 jit_solution(7167523087642346681)
XLA Ops:
  0.0 50.0 %waves.1.rho_ref = bf16[512,384]{1,0:T(8,128)(2,1)} custom-call(f32[32,1,1024]{2,1,0:T(1,128)} %wannier_ref.1, s32[2,384]{1,0:T(2,128)} %bitcast.3, s32[64,128]{1,0:T(8,128)} %bitcast.2), custom_call_target="tpu_custom_call" | custom-call | tf_op jit(solution)/shard_map/waves/pallas_call | solution.py:483
  50.0 101.2 %matrix.1 = f32[2,2,12,384]{3,2,1,0:T(8,128)} custom-call(bf16[512,384]{1,0:T(8,128)(2,1)} %waves.1.rho_ref, bf16[2,2,512,4096]{3,2,1,0:T(8,128)(2,1)} %w_hbm.1), custom_call_target="tpu_custom_call" | custom-call | tf_op jit(solution)/shard_map/matrix/pallas_call | solution.py:506
  151.2 1.6 %copy.5 = f32[2,2,12,384]{3,1,2,0:T(2,128)} copy(f32[2,2,12,384]{3,2,1,0:T(8,128)} %matrix.1) | data formatting | bytes 147456 | tf_op jit(solution)/shard_map/matrix/pallas_call | solution.py:506

commit v4 on v3

--- a/solution.py
+++ b/solution.py
@@ -64,21 +64,25 @@
         if before is not None:
             before()
 
+        def forward(chunk, step, ways):
+            for way in range(2):
+                self.copy(way, chunk, step - 1, False, True).wait_recv()
+                if way in ways:
+                    self.copy(way, chunk, step, False).start()
+
+        for chunk in range(2):
+            forward(chunk, 1, (0, 1))
+
         def step_body(step, _):
             for chunk in range(2):
-                for way in range(2):
-                    self.copy(way, chunk, step - 1, False, True).wait_recv()
-                    self.copy(way, chunk, step, False).start()
-            on_block(self.owner(0, step))
-            on_block(self.owner(1, step))
+                forward(chunk, step, (0, 1))
+                on_block(self.owner(chunk, step - 1))
             return 0
 
-        lax.fori_loop(1, last, step_body, 0)
+        lax.fori_loop(2, last, step_body, 0)
         for chunk in range(2):
-            for way in range(2):
-                self.copy(way, chunk, last - 1, False, True).wait_recv()
-                if way == chunk:
-                    self.copy(way, chunk, last, False).start()
+            forward(chunk, last, (chunk,))
+            on_block(self.owner(chunk, last - 1))
         on_block(self.owner(0, last))
         on_block(self.owner(1, last))
         for way in range(2):
@@ -372,7 +376,6 @@
 
     ring = Ring(n, rho_ref, lambda owner: panel.at[owner], send_sems, recv_sems)
     ring.run(on_block, before)
-    ring.drain()
 
     @pl.when(holds_left)
     def _():
@@ -403,6 +406,7 @@
     pair_out[...] = elements(1 - col).astype(BF16)
     pair_copy.start()
     value = elements(col)
+    ring.drain()
     pair_copy.wait()
     value = value + pair_in[...].astype(F32)
     share = pairs // n

time: 153 us -> 153 us (level)
  no operation moved by 1% of the time
where the time goes in v4:
time: 153 us
  Pallas kernels  151 us (99%)
  local copies, waits for them, and re-layouts  1.56 us (1%)
    pallas_call x1, Pallas kernels, shards(): pl.pallas_call(functools.partial(matrix_kernel, n, 1.0 / math.sqrt(gmap.s...  101 us
    pallas_call x1, Pallas kernels, shards(): pl.pallas_call(functools.partial(wave_kernel, n), out_shape=jax.ShapeDtyp...  50 us

profile of v4, /device:TPU:69, one launch (start us, length us, event | category | flops | bytes accessed | tf_op | source)
XLA Modules:
  0.0 152.7 jit_solution(4783795313133967876)
XLA Ops:
  0.0 50.0 %waves.1.rho_ref = bf16[512,384]{1,0:T(8,128)(2,1)} custom-call(f32[32,1,1024]{2,1,0:T(1,128)} %wannier_ref.1, s32[2,384]{1,0:T(2,128)} %bitcast.3, s32[64,128]{1,0:T(8,128)} %bitcast.2), custom_call_target="tpu_custom_call" | custom-call | tf_op jit(solution)/shard_map/waves/pallas_call | solution.py:487
  50.0 101.1 %matrix.1 = f32[2,2,12,384]{3,2,1,0:T(8,128)} custom-call(bf16[512,384]{1,0:T(8,128)(2,1)} %waves.1.rho_ref, bf16[2,2,512,4096]{3,2,1,0:T(8,128)(2,1)} %w_hbm.1), custom_call_target="tpu_custom_call" | custom-call | tf_op jit(solution)/shard_map/matrix/pallas_call | solution.py:510
  151.1 1.6 %copy.5 = f32[2,2,12,384]{3,1,2,0:T(2,128)} copy(f32[2,2,12,384]{3,2,1,0:T(8,128)} %matrix.1) | data formatting | bytes 147456 | tf_op jit(solution)/shard_map/matrix/pallas_call | solution.py:510
